TPU v7x, 256 devices: a whole 4x4x8 slice. The times are simulated.
256 devices in a mesh: row: 32 (over y, x, core), col: 8 (over z).
Axes of the slice: x: 4, y: 4, z: 8, core: 2. Of those that a mesh axis runs over, the one named last changes fastest.
Arguments:
- vectors_window: float32 [32, 32, 64, 1024], P(None, 'row', None, 'col'), may hold values from -6 to 6
- column_strip: float32 [32, 32, 64, 1024], P(None, 'row', None, 'col'), may hold values from -6 to 6
- row_strip: float32 [1024, 64, 8, 128], P('row', None, 'col'), may hold values from -6 to 6
- factor: float32 [1024, 1024], P('row', 'col'), may hold values from -2 to 2
- window_start: int32 [1], replicated, may hold values from 1 to 64512
- deflated: int32 [1], replicated, may hold values from 0 to 512
Outputs:
- vectors_updated: float32 [32, 32, 64, 1024], P(None, 'row', None, 'col')
- column_updated: float32 [32, 32, 64, 1024], P(None, 'row', None, 'col')
- row_updated: float32 [1024, 64, 8, 128], P('row', None, 'col')
All inputs are finite; a program needn't handle non-finite values.
Results may differ from a plain program's by a relative error of at most 0.0003.
Values sent between devices are 32-bit elements; how exact they have to be, the bound alone decides.
A program may use at most 64 MiB of HBM per device.

v0:
```python
import jax
import jax.numpy as jnp
from jax import lax
from jax.sharding import PartitionSpec as P

W = 1024


def from_everyone(x, axis):
    peers = lax.axis_size(axis)
    return lax.all_to_all(jnp.broadcast_to(x[None], (peers, *x.shape)), axis, 0, 0, tiled=True)


def laid_out(pieces, dim):
    dims = list(pieces.shape[1:])
    dims[dim] *= pieces.shape[0]
    return jnp.moveaxis(pieces, 0, dim).reshape(dims)


def gather_directly(x, axis, dim):
    pieces = from_everyone(x, axis)
    return laid_out(pieces, dim)


def reflect(factor, deflated):
    columns = jnp.arange(W, dtype=jnp.int32)
    kept_count = W - deflated[0]
    spike_row = jnp.where(columns < kept_count, factor[0], 0.0)
    squares = jnp.sum(spike_row * spike_row)
    corner = factor[0, 0]
    magnitude = jnp.sqrt(squares + 1e-06)
    signum = jnp.where(corner >= 0, 1.0, -1.0)
    vector = spike_row + jnp.where(columns == 0, signum * magnitude, 0.0)
    denominator = squares + 2.0 * jnp.abs(corner) * magnitude + magnitude * magnitude
    scaling = 2.0 / denominator
    reflected_image = jnp.dot(factor, vector, precision=lax.Precision.HIGHEST)
    return factor - scaling * reflected_image[:, None] * vector[None, :]


def body(vectors_window, column_strip, row_strip, factor, window_start, deflated):
    highest = lax.Precision.HIGHEST
    row_position = lax.axis_index("row")
    column_position = lax.axis_index("col")
    start_row = window_start[0]
    widened = gather_directly(factor, "col", 1)
    rotation = reflect(lax.all_gather(widened, "row", axis=0, tiled=True), deflated)
    rounds = vectors_window.shape[0]
    blocks = vectors_window.shape[2]
    local_width = vectors_window.shape[3]
    z_blocks = vectors_window.reshape(rounds, blocks, local_width)
    strip_blocks = column_strip.reshape(rounds, blocks, local_width)
    z_turned = jnp.einsum(
        "rbk,kj->rbj",
        lax.all_to_all(z_blocks, "col", split_axis=1, concat_axis=2, tiled=True),
        rotation,
        precision=highest,
    )
    strip_turned = jnp.einsum(
        "rbk,kj->rbj",
        lax.all_to_all(strip_blocks, "col", split_axis=1, concat_axis=2, tiled=True),
        rotation,
        precision=highest,
    )
    z_rotated = lax.all_to_all(z_turned, "col", split_axis=2, concat_axis=1, tiled=True)
    strip_rotated = lax.all_to_all(strip_turned, "col", split_axis=2, concat_axis=1, tiled=True)
    row_count = lax.axis_size("row")
    round_number = jnp.arange(rounds, dtype=jnp.int32)[:, None]
    block_number = jnp.arange(blocks, dtype=jnp.int32)[None, :]
    row_number = (round_number * row_count + row_position) * blocks + block_number
    column_updated = jnp.where(
        row_number[:, :, None] < start_row, strip_rotated, strip_blocks
    ).reshape(column_strip.shape)
    vectors_updated = z_rotated.reshape(vectors_window.shape)
    strip_rows = row_strip.shape[0]
    flat_strip = row_strip.reshape(strip_rows, -1)
    stacked = lax.all_to_all(flat_strip, "row", split_axis=1, concat_axis=0, tiled=True)
    rotated_rows = lax.dot_general(rotation, stacked, (((0,), (0,)), ((), ())), precision=highest)
    returned = lax.all_to_all(rotated_rows, "row", split_axis=0, concat_axis=1, tiled=True)
    column_count = lax.axis_size("col")
    column_rounds = row_strip.shape[1]
    column_block = row_strip.shape[3]
    round_index = jnp.arange(column_rounds, dtype=jnp.int32)[:, None]
    lane_index = jnp.arange(column_block, dtype=jnp.int32)[None, :]
    column_number = (round_index * column_count + column_position) * column_block + lane_index
    row_updated = jnp.where(
        column_number[None, :, None, :] >= start_row + W,
        returned.reshape(row_strip.shape),
        row_strip,
    )
    return (vectors_updated, column_updated, row_updated)


def solution(mesh):
    return jax.shard_map(
        body,
        mesh=mesh,
        in_specs=(
            P(None, "row", None, "col"),
            P(None, "row", None, "col"),
            P("row", None, "col", None),
            P("row", "col"),
            P(),
            P(),
        ),
        out_specs=(
            P(None, "row", None, "col"),
            P(None, "row", None, "col"),
            P("row", None, "col", None),
        ),
        check_vma=False,
    )
```

profile of v0, /device:TPU:1, one launch (start us, length us, event | category | flops | bytes accessed | tf_op | source)
XLA Modules:
  0.0 231.8 jit_solution(5835078651876137352)
XLA Ops:
  7.2 0.0 all-gather.2.cloned.1.call-start
  7.2 0.7 broadcast_in_dim.44
  7.9 16.6 %all_to_all.106 = f32[8,32,128]{2,1,0:T(8,128)S(1)} all-to-all(f32[8,32,128]{2,1,0:T(8,128)S(1)} %broadcast_in_dim.44), channel_id=1, replica_groups=mesh['row'=32,'col'=8] {'col'}, dimensions={0} | all-to-all | bytes 262144 | tf_op jit(solution)/shard_map/all_to_all | solution.py:11
  24.5 0.7 copy_bitcast_fusion.4
  25.2 0.0 all-gather.2.cloned.1.call-update
  25.2 0.5 broadcast.101
  25.7 4.4 %reduce.3 = f32[32,64,128]{2,1,0:T(8,128)S(1)} reduce(f32[32,64,1,128]{3,2,1,0:T(1,128)} %param.8, f32[]{:T(128)} %broadcast.101), dimensions={2}, to_apply=%param.8.reduce_sub_computation.3 | reduce | bytes 2097156 | tf_op args[2]
  30.2 0.3 all_to_all.93
  30.5 0.0 copy-start.2
  30.5 1.6 copy.61
  32.0 9.4 %all-to-all-start.5 = ((f32[32,32,256]{2,0,1:T(8,128)}), f32[32,32,256]{2,0,1:T(8,128)S(1)}, u32[]{:S(2)}, u32[]{:S(2)}) async-start(f32[32,32,256]{2,0,1:T(8,128)} %copy.61), calls=%async_computation.5 | async-start | bytes 2097152 | tf_op jit(solution)/shard_map/all_to_all | solution.py:76
  41.4 2.8 %copy.74 = f32[32,1,64,128]{3,0,2,1:T(8,128)} copy(f32[32,1,64,128]{3,2,1,0:T(8,128)} %param.6) | data formatting | bytes 2097152 | tf_op args[0]
  44.2 14.1 %all-to-all-done.5 = f32[32,32,256]{2,0,1:T(8,128)S(1)} async-done(((f32[32,32,256]{2,0,1:T(8,128)}), f32[32,32,256]{2,0,1:T(8,128)S(1)}, u32[]{:S(2)}, u32[]{:S(2)}) %all-to-all-start.5) | async-done | bytes 1048608 | tf_op jit(solution)/shard_map/all_to_all | solution.py:76
  58.4 3.6 %all-to-all-start.1 = ((f32[32,64,128]{2,0,1:T(8,128)}), f32[32,64,128]{2,0,1:T(8,128)S(1)}, u32[]{:S(2)}, u32[]{:S(2)}) async-start(f32[32,64,128]{2,0,1:T(8,128)} %bitcast.78), calls=%async_computation.1 | async-start | bytes 2097152 | tf_op jit(solution)/shard_map/all_to_all | solution.py:54
  62.6 0.0 copy-done.2
  62.7 1.6 copy.72
  64.2 16.0 %all-gather.2.cloned.1.call-done = f32[1024,1024]{1,0:T(8,128)} async-done(((f32[32,1024]{1,0:T(8,128)}), f32[1024,1024]{1,0:T(8,128)}) %all-gather.2.cloned.1.call-update) | async-done | bytes 4194320 | tf_op jit(solution)/shard_map/all_gather | solution.py:46
  80.3 0.8 slice.8
  81.0 10.2 %all-to-all-done.1 = f32[32,64,128]{2,0,1:T(8,128)S(1)} async-done(((f32[32,64,128]{2,0,1:T(8,128)}), f32[32,64,128]{2,0,1:T(8,128)S(1)}, u32[]{:S(2)}, u32[]{:S(2)}) %all-to-all-start.1) | async-done | bytes 1048608 | tf_op jit(solution)/shard_map/all_to_all | solution.py:54
  91.2 3.7 %all-to-all-start.3 = ((f32[32,64,128]{2,0,1:T(8,128)}), f32[32,64,128]{2,0,1:T(8,128)S(1)}, u32[]{:S(2)}, u32[]{:S(2)}) async-start(f32[32,64,128]{2,0,1:T(8,128)} %bitcast.76), calls=%async_computation.3 | async-start | bytes 2097152 | tf_op jit(solution)/shard_map/all_to_all | solution.py:60
  94.9 0.6 multiply_reduce_fusion
  95.5 1.2 slice.9
  99.4 0.0 copy-start
  99.4 5.8 %fusion.17 = f32[1,1024]{1,0:T(1,128)S(1)} fusion(f32[1024,1]{0,1:T(1,128)S(1)} %bitcast.101, f32[1024,1024]{1,0:T(8,128)} %all-gather.2.cloned.1.call-done), kind=kOutput, calls=%fused_computation.32 | convolution fusion | flops 12582912 | bytes 4202496 | tf_op jit(solution)/shard_map/dot_general | solution.py:36
  105.2 0.0 copy-done
  105.3 2.4 %fusion.4 = f32[1024,1024]{0,1:T(8,128)} fusion(f32[1024,1024]{1,0:T(8,128)S(1)} %copy-done, f32[1024]{0:T(1024)S(1)} %bitcast.97, f32[1024]{0:T(1024)S(1)} %broadcast_multiply_fusion), kind=kLoop, calls=%fused_computation.5 | loop fusion | flops 2097152 | bytes 8396800 | tf_op jit(solution)/shard_map/dot_general | solution.py:77
  107.6 5.4 %copy.60 = f32[1024,1024]{1,0:T(8,128)} copy(f32[1024,1024]{0,1:T(8,128)} %fusion.4) | data formatting | bytes 8388608 | tf_op jit(solution)/shard_map/dot_general | solution.py:77
  113.0 6.6 %fusion.18 = f32[32,32,256]{2,1,0:T(8,128)} fusion(f32[32,32,1024]{2,1,0:T(8,128)} %bitcast.85, f32[1024,256,1]{1,0,2:T(8,128)S(1)} %bitcast.92), kind=kOutput, calls=%fused_computation.33 | convolution fusion | flops 3221225472 | bytes 6291456 | tf_op jit(solution)/shard_map/dot_general | solution.py:77
  119.6 2.3 %all-to-all-done.3 = f32[32,64,128]{2,0,1:T(8,128)S(1)} async-done(((f32[32,64,128]{2,0,1:T(8,128)}), f32[32,64,128]{2,0,1:T(8,128)S(1)}, u32[]{:S(2)}, u32[]{:S(2)}) %all-to-all-start.3) | async-done | bytes 1048608 | tf_op jit(solution)/shard_map/all_to_all | solution.py:60
  121.9 5.0 %all-to-all-start.6 = ((f32[32,32,256]{2,1,0:T(8,128)}), f32[32,32,256]{2,1,0:T(8,128)S(1)}, u32[]{:S(2)}, u32[]{:S(2)}) async-start(f32[32,32,256]{2,1,0:T(8,128)} %fusion.18), calls=%async_computation.6 | async-start | bytes 2097152 | tf_op jit(solution)/shard_map/all_to_all | solution.py:78
  126.9 1.6 copy.73
  128.5 2.4 %all_to_all.81 = f32[32,8,1024]{2,0,1:T(8,128)} reshape(f32[32,8,8,128]{3,2,0,1:T(8,128)} %bitcast.90) | data formatting | bytes 2097152 | tf_op jit(solution)/shard_map/all_to_all | solution.py:54
  130.8 6.4 %fusion.9 = f32[32,8,1024]{2,0,1:T(8,128)S(1)} fusion(f32[32,8,1024]{2,0,1:T(8,128)} %all_to_all.81, f32[1024,1024]{1,0:T(8,128)} %all-gather.2.cloned.1.call-done, f32[1024]{0:T(1024)S(1)} %bitcast.98, f32[1024]{0:T(1024)S(1)} %broadcast_multiply_fusion), kind=kOutput, calls=%fused_computation.10 | convolution fusion | flops 3223322624 | bytes 6299648 | tf_op jit(solution)/shard_map/rbk,kj->rbj/dot_general | solution.py:52
  137.2 2.7 %copy.54 = f32[32,8,1024]{0,1,2:T(8,128)} copy(f32[32,8,1024]{2,0,1:T(8,128)S(1)} %fusion.9) | data formatting | bytes 2097152 | tf_op jit(solution)/shard_map/rbk,kj->rbj/dot_general | solution.py:52
  140.0 4.8 %reshape.143 = f32[8,1,32768]{2,1,0:T(1,128)} reshape(f32[1024,8,32]{2,1,0:T(8,128)} %bitcast.81) | data formatting | bytes 2097152
  144.8 0.0 all-to-all-done.6
  144.8 0.0 copy-start.4
  144.8 1.0 copy-done.4
  145.8 4.3 %all-to-all-start.2 = ((f32[8,1,32768]{2,1,0:T(1,128)}), f32[8,1,32768]{2,1,0:T(1,128)S(1)}, u32[]{:S(2)}, u32[]{:S(2)}) async-start(f32[8,1,32768]{2,1,0:T(1,128)} %reshape.143), calls=%async_computation.2 | async-start | bytes 2097152 | tf_op jit(solution)/shard_map/all_to_all | solution.py:64
  150.1 0.6 copy.71
  150.7 1.1 all_to_all.88
  151.8 6.4 %fusion.12 = f32[32,8,1024]{2,0,1:T(8,128)S(1)} fusion(f32[32,8,1024]{2,0,1:T(8,128)} %all_to_all.88, f32[1024,1024]{1,0:T(8,128)} %all-gather.2.cloned.1.call-done, f32[1024]{0:T(1024)S(1)} %bitcast.99, f32[1024]{0:T(1024)S(1)} %broadcast_multiply_fusion), kind=kOutput, calls=%fused_computation.11 | convolution fusion | flops 3223322624 | bytes 6299648 | tf_op jit(solution)/shard_map/rbk,kj->rbj/dot_general | solution.py:58
  158.2 2.7 %copy.58 = f32[32,8,1024]{0,1,2:T(8,128)} copy(f32[32,8,1024]{2,0,1:T(8,128)S(1)} %fusion.12) | data formatting | bytes 2097152 | tf_op jit(solution)/shard_map/rbk,kj->rbj/dot_general | solution.py:58
  160.9 4.9 %reshape.145 = f32[8,1,32768]{2,1,0:T(1,128)} reshape(f32[1024,8,32]{2,1,0:T(8,128)} %bitcast.82) | data formatting | bytes 2097152
  165.9 13.5 %all-to-all-done.2 = f32[8,1,32768]{2,1,0:T(1,128)S(1)} async-done(((f32[8,1,32768]{2,1,0:T(1,128)}), f32[8,1,32768]{2,1,0:T(1,128)S(1)}, u32[]{:S(2)}, u32[]{:S(2)}) %all-to-all-start.2) | async-done | bytes 1048608 | tf_op jit(solution)/shard_map/all_to_all | solution.py:64
  179.3 4.2 %all-to-all-start.4 = ((f32[8,1,32768]{2,1,0:T(1,128)}), f32[8,1,32768]{2,1,0:T(1,128)}, u32[]{:S(2)}, u32[]{:S(2)}) async-start(f32[8,1,32768]{2,1,0:T(1,128)} %reshape.145), calls=%async_computation.4 | async-start | bytes 2097152 | tf_op jit(solution)/shard_map/all_to_all | solution.py:65
  184.3 0.1 add_compare_fusion.1
  184.3 0.1 add_compare_fusion
  184.4 0.0 copy-done.5
  184.4 1.6 copy.62
  186.0 1.3 reshape.129
  187.3 0.0 copy-done.1
  187.3 1.1 broadcast_select_fusion
  188.4 0.5 broadcast.102
  189.0 3.1 %reduce.4 = f32[8,32768]{1,0:T(8,128)S(1)} reduce(f32[8,1,32768]{2,1,0:T(1,128)S(1)} %all-to-all-done.2, f32[]{:T(128)} %broadcast.102), dimensions={1}, to_apply=%all_to_all.82.reduce_sub_computation | reduce | bytes 2097156 | tf_op jit(solution)/shard_map/all_to_all | solution.py:64
  192.0 3.3 %reshape.144 = f32[1024,8,32]{2,1,0:T(8,128)} reshape(f32[8,32768]{1,0:T(8,128)S(1)} %reduce.4) | data formatting | bytes 2097152
  195.3 3.9 %copy.55 = f32[32,8,8,128]{3,2,1,0:T(8,128)} copy(f32[32,8,8,128]{0,2,3,1:T(8,128)} %bitcast.83) | data formatting | bytes 2097152 | tf_op jit(solution)/shard_map/all_to_all | solution.py:64
  199.3 13.5 %all-to-all-done.4 = f32[8,1,32768]{2,1,0:T(1,128)} async-done(((f32[8,1,32768]{2,1,0:T(1,128)}), f32[8,1,32768]{2,1,0:T(1,128)}, u32[]{:S(2)}, u32[]{:S(2)}) %all-to-all-start.4) | async-done | bytes 1048608 | tf_op jit(solution)/shard_map/all_to_all | solution.py:65
  212.8 4.3 %reduce.5 = f32[8,32768]{1,0:T(8,128)S(1)} reduce(f32[8,1,32768]{2,1,0:T(1,128)} %all-to-all-done.4, f32[]{:T(128)} %broadcast.102), dimensions={1}, to_apply=%all_to_all.89.reduce_sub_computation | reduce | bytes 2097156 | tf_op jit(solution)/shard_map/all_to_all | solution.py:65
  217.1 0.0 copy-start.3
  217.1 3.3 %reshape.146 = f32[1024,8,32]{2,1,0:T(8,128)} reshape(f32[8,32768]{1,0:T(8,128)S(1)} %reduce.5) | data formatting | bytes 2097152
  220.4 3.2 %copy.59 = f32[32,8,8,128]{3,2,1,0:T(8,128)S(1)} copy(f32[32,8,8,128]{0,2,3,1:T(8,128)} %bitcast.84) | data formatting | bytes 2097152 | tf_op jit(solution)/shard_map/all_to_all | solution.py:65
  223.6 0.0 copy-done.3
  223.7 1.3 bitcast_select_fusion
  (7 shorter events, 0.0 us)
Async XLA Ops:
  7.2 73.1 %all-gather.2.cloned.1.call-start = ((), (), s32[]{:S(2)}) async-start(), calls=%async_computation.7 | async-start | bytes 4325376 | tf_op jit(solution)/shard_map/all_gather | solution.py:46
  30.5 32.2 %copy-start.2 = (f32[32,1,64,128]{3,2,1,0:T(8,128)S(1)}, f32[32,1,64,128]{3,2,1,0:T(8,128)}, u32[]{:S(2)}) copy-start(f32[32,1,64,128]{3,2,1,0:T(8,128)} %param.7) | copy-start | bytes 3145732
  32.0 26.3 %all-to-all-start.5 = ((f32[32,32,256]{2,0,1:T(8,128)}), f32[32,32,256]{2,0,1:T(8,128)S(1)}, u32[]{:S(2)}, u32[]{:S(2)}) async-start(f32[32,32,256]{2,0,1:T(8,128)} %copy.61), calls=%async_computation.5 | async-start | bytes 2097152 | tf_op jit(solution)/shard_map/all_to_all | solution.py:76
  58.4 32.8 %all-to-all-start.1 = ((f32[32,64,128]{2,0,1:T(8,128)}), f32[32,64,128]{2,0,1:T(8,128)S(1)}, u32[]{:S(2)}, u32[]{:S(2)}) async-start(f32[32,64,128]{2,0,1:T(8,128)} %bitcast.78), calls=%async_computation.1 | async-start | bytes 2097152 | tf_op jit(solution)/shard_map/all_to_all | solution.py:54
  91.2 30.7 %all-to-all-start.3 = ((f32[32,64,128]{2,0,1:T(8,128)}), f32[32,64,128]{2,0,1:T(8,128)S(1)}, u32[]{:S(2)}, u32[]{:S(2)}) async-start(f32[32,64,128]{2,0,1:T(8,128)} %bitcast.76), calls=%async_computation.3 | async-start | bytes 2097152 | tf_op jit(solution)/shard_map/all_to_all | solution.py:60
  99.4 5.8 %copy-start = (f32[1024,1024]{1,0:T(8,128)S(1)}, f32[1024,1024]{1,0:T(8,128)}, u32[]{:S(2)}) copy-start(f32[1024,1024]{1,0:T(8,128)} %all-gather.2.cloned.1.call-done) | copy-start | bytes 12582916
  121.9 22.9 %all-to-all-start.6 = ((f32[32,32,256]{2,1,0:T(8,128)}), f32[32,32,256]{2,1,0:T(8,128)S(1)}, u32[]{:S(2)}, u32[]{:S(2)}) async-start(f32[32,32,256]{2,1,0:T(8,128)} %fusion.18), calls=%async_computation.6 | async-start | bytes 2097152 | tf_op jit(solution)/shard_map/all_to_all | solution.py:78
  144.8 1.0 copy-start.4
  145.8 33.6 %all-to-all-start.2 = ((f32[8,1,32768]{2,1,0:T(1,128)}), f32[8,1,32768]{2,1,0:T(1,128)S(1)}, u32[]{:S(2)}, u32[]{:S(2)}) async-start(f32[8,1,32768]{2,1,0:T(1,128)} %reshape.143), calls=%async_computation.2 | async-start | bytes 2097152 | tf_op jit(solution)/shard_map/all_to_all | solution.py:64
  160.9 23.5 %copy-start.5 = (f32[32,32,256]{2,1,0:T(8,128)S(1)}, f32[32,32,256]{2,1,0:T(8,128)}, u32[]{:S(2)}) copy-start(f32[32,32,256]{2,1,0:T(8,128)} %copy-done.4) | copy-start | bytes 3145732
  165.9 21.5 %copy-start.1 = (f32[32,64,1,128]{3,2,1,0:T(1,128)S(1)}, f32[32,64,1,128]{3,2,1,0:T(1,128)}, u32[]{:S(2)}) copy-start(f32[32,64,1,128]{3,2,1,0:T(1,128)} %param.8) | copy-start | bytes 3145732
  179.3 33.5 %all-to-all-start.4 = ((f32[8,1,32768]{2,1,0:T(1,128)}), f32[8,1,32768]{2,1,0:T(1,128)}, u32[]{:S(2)}, u32[]{:S(2)}) async-start(f32[8,1,32768]{2,1,0:T(1,128)} %reshape.145), calls=%async_computation.4 | async-start | bytes 2097152 | tf_op jit(solution)/shard_map/all_to_all | solution.py:65
  217.1 6.5 %copy-start.3 = (f32[32,1,64,128]{3,2,1,0:T(8,128)S(1)}, f32[32,1,64,128]{3,2,1,0:T(8,128)}, u32[]{:S(2)}) copy-start(f32[32,1,64,128]{3,2,1,0:T(8,128)} %param.7) | copy-start | bytes 3145732
Sparse Core Ops, SparseCore 0:
  25.3 54.9 all-gather.1
where the time goes:
time: 233 us; the launch traced here: 232 us
  waiting for transfers between devices  69.7 us (30%)
  local copies, waits for them, and re-layouts  54.5 us (23%)
  starting transfers between devices  30.3 us (13%)
  matrix products  25.2 us (11%)
  between operations  18.2 us (8%)
  other arithmetic  17.4 us (7%)
  blocking collectives  16.6 us (7%)
    unnamed x19, local copies, waits for them, and re-layouts  22.3 us
    all_to_all x1, blocking collectives, from_everyone(): lax.all_to_all(jnp.broadcast_to(x[None], (peers, *x.shape)), axis, 0, 0,...  16.6 us
    all_gather x1, waiting for transfers between devices, body(): lax.all_gather(widened, 'row', axis=0, tiled=True)  16 us
    all_to_all x1, waiting for transfers between devices, body(): lax.all_to_all(flat_strip, 'row', split_axis=1, concat_axis=0, tiled=True)  14.1 us
    all_to_all x1, waiting for transfers between devices, body(): lax.all_to_all(strip_turned, 'col', split_axis=2, concat_axis=1, tiled=True)  13.5 us
    all_to_all x1, waiting for transfers between devices, body(): lax.all_to_all(z_turned, 'col', split_axis=2, concat_axis=1, tiled=True)  13.5 us
    all_to_all x1, waiting for transfers between devices, body(): lax.all_to_all(z_blocks, 'col', split_axis=1, concat_axis=2, tiled=True)  10.2 us
    all_to_all x1, starting transfers between devices, body(): lax.all_to_all(flat_strip, 'row', split_axis=1, concat_axis=0, tiled=True)  9.38 us
  transfers between devices with their start and end apart: 7, of which 6 were waited for; matrix products, arithmetic and copies ran while one was open for 34% of the time, Pallas kernels for 0%

commit v1 on v0

v1 whole, which is shorter than its diff:
```python
import functools

import jax
import jax.numpy as jnp
from jax import lax
from jax.experimental import pallas as pl
from jax.experimental.pallas import tpu as pltpu
from jax.sharding import PartitionSpec as P

W = 1024
Z = 8
ROWS = 32
CHUNK = 64
MESH = pl.DeviceIdType.MESH


def send(src, dst, sent, landed, device):
    pltpu.make_async_remote_copy(
        src_ref=src, dst_ref=dst, send_sem=sent, recv_sem=landed, device_id=device, device_id_type=MESH
    ).start()


def drain(ref, semaphore):
    pltpu.make_async_copy(ref, ref, semaphore).wait()


def lanes(index, size=128):
    return pl.ds(pl.multiple_of(index * size, size), size)


def row_of(y, x, core):
    return (y * 4 + x) * 2 + core


def rotate(x, high, low, store):
    rows = x.shape[0]
    x_high = x.astype(jnp.bfloat16)
    x_low = (x - x_high.astype(jnp.float32)).astype(jnp.bfloat16)
    both = jnp.concatenate([x_high, x_low], axis=0)
    for n in range(4):
        columns = slice(256 * n, 256 * n + 256)
        top = jnp.dot(both, high[:, columns], preferred_element_type=jnp.float32)
        bottom = jnp.dot(x_high, low[:, columns], preferred_element_type=jnp.float32)
        store(columns, top[:rows] + top[rows:] + bottom)


def kernel(
    chunks, per_device, first_round,
    deflated, f_ref, z_ref, c_ref, s_ref,
    zo_ref, co_ref, so_ref,
    factor, high, low, z_in, c_in, z_out, c_out, s_in, s_out, s_turned, s_rotated,
    local, f_sent, f_landed, ring_sent, ring_landed, far_sent, far_landed, pair_sent, pair_landed,
    in_sent, z_landed, c_landed, out_sent, zo_landed, co_landed, s_sent, s_landed, so_sent, so_landed,
):
    row = lax.axis_index("row")
    mine = lax.axis_index("col")
    y, x, core = row // 8, (row // 2) % 4, row % 2
    barrier = pltpu.get_barrier_semaphore()

    @pl.loop(1, Z)
    def _(d):
        pl.semaphore_signal(barrier, inc=1, device_id=(row, (mine + d) % Z), device_id_type=MESH)

    @pl.loop(1, ROWS)
    def _(d):
        pl.semaphore_signal(barrier, inc=1, device_id=((row + d) % ROWS, mine), device_id_type=MESH)

    own = [
        pltpu.make_async_copy(f_ref, factor.at[y, x, core, :, lanes(mine)], local.at[0]),
        pltpu.make_async_copy(z_ref.at[:, mine], z_in.at[:, :, lanes(mine)], local.at[1]),
        pltpu.make_async_copy(c_ref.at[0:chunks, mine], c_in.at[0:chunks, :, lanes(mine)], local.at[2]),
    ]
    for copy in own:
        copy.start()
    pl.semaphore_wait(barrier, Z - 1 + ROWS - 1)

    far_first = (4, 3, 5, 2, 6, 1, 7)
    for d in far_first:
        peer = (row, (mine + d) % Z)
        send(f_ref, factor.at[y, x, core, :, lanes(mine)], f_sent, f_landed, peer)
    for d in far_first:
        other = (mine + d) % Z
        send(z_ref.at[:, other], z_in.at[:, :, lanes(mine)], in_sent.at[0], z_landed, (row, other))
    for d in far_first:
        other = (mine + d) % Z
        send(
            c_ref.at[0:chunks, other], c_in.at[0:chunks, :, lanes(mine)],
            in_sent.at[1], c_landed, (row, other),
        )

    own[0].wait()
    drain(factor.at[0, 0, 0, :, 0:896], f_landed)
    left, right = slice(0, 512), slice(512, 1024)
    for d in (2, 1, 3):
        piece = factor.at[y, x, core, :, left]
        send(piece, piece, ring_sent.at[0], ring_landed.at[0], (row_of(y, (x + d) % 4, core), mine))
        piece = factor.at[y, x, core, :, right]
        send(piece, piece, ring_sent.at[1], ring_landed.at[1], (row_of((y + d) % 4, x, core), mine))
    drain(factor.at[0, 0:3, 0, :, left], ring_landed.at[0])
    line_x = factor.at[y, :, core, :, left]
    for d in (2, 1, 3):
        send(line_x, line_x, far_sent.at[0], far_landed.at[0, d], (row_of((y + d) % 4, x, core), mine))
    drain(factor.at[0:3, 0, 0, :, right], ring_landed.at[1])
    line_y = factor.at[:, x, core, :, right]
    for d in (2, 1, 3):
        send(line_y, line_y, far_sent.at[1], far_landed.at[1, d], (row_of(y, (x + d) % 4, core), mine))

    partner = (row_of(y, x, 1 - core), mine)
    send(line_x, line_x, pair_sent, pair_landed, partner)
    send(line_y, line_y, pair_sent, pair_landed, partner)

    @pl.loop(1, ROWS)
    def _(d):
        other = (row + d) % ROWS
        for e in range(per_device):
            send(
                s_ref.at[:, first_round + other * per_device + e],
                s_in.at[e, pl.ds(row * 32, 32)],
                s_sent, s_landed, (other, mine),
            )

    own_rounds = [
        pltpu.make_async_copy(
            s_ref.at[:, first_round + row * per_device + e], s_in.at[e, pl.ds(row * 32, 32)], local.at[3 + e]
        )
        for e in range(per_device)
    ]
    for copy in own_rounds:
        copy.start()

    for d in (1, 3, 2):
        piece = factor.at[(y + 4 - d) % 4, :, core, :, left]
        drain(piece, far_landed.at[0, d])
        send(piece, piece, pair_sent, pair_landed, partner)
        piece = factor.at[:, (x + 4 - d) % 4, core, :, right]
        drain(piece, far_landed.at[1, d])
        send(piece, piece, pair_sent, pair_landed, partner)
    drain(factor.at[:, :, 0], pair_landed)

    spike = factor[0, 0, 0, 0:1, :]
    columns = lax.broadcasted_iota(jnp.int32, (1, W), 1)
    spike_row = jnp.where(columns < W - deflated[0], spike, 0.0)
    squares = jnp.sum(spike_row * spike_row, axis=1, keepdims=True)
    corner = spike[:, 0:1]
    magnitude = jnp.sqrt(squares + 1e-06)
    signum = jnp.where(corner >= 0, 1.0, -1.0)
    vector = spike_row + jnp.where(columns == 0, signum * magnitude, 0.0)
    denominator = squares + 2.0 * jnp.abs(corner) * magnitude + magnitude * magnitude
    scaling = 2.0 / denominator

    @pl.loop(0, ROWS)
    def _(b):
        block = factor[b // 8, (b // 2) % 4, b % 2]
        image = jnp.sum(block * vector, axis=1, keepdims=True)
        turned = block - (scaling * image) * vector
        top = turned.astype(jnp.bfloat16)
        high[pl.ds(pl.multiple_of(b * 32, 32), 32), :] = top
        low[pl.ds(pl.multiple_of(b * 32, 32), 32), :] = (turned - top.astype(jnp.float32)).astype(jnp.bfloat16)

    def turn(count, source, result, target, sent, landed):
        @pl.loop(0, count)
        def _(c):
            def store(columns, value):
                result[c, :, columns] = value

            rotate(source[c], high, low, store)
            for d in far_first:
                other = (mine + d) % Z
                send(result.at[c, :, lanes(other)], target.at[c, mine], sent, landed, (row, other))
            pltpu.make_async_copy(result.at[c, :, lanes(mine)], target.at[c, mine], local.at[5]).start()

    own[1].wait()
    drain(z_in.at[:, :, 0:896], z_landed)
    turn(4, z_in, z_out, zo_ref, out_sent.at[0], zo_landed)
    drain(z_out.at[:, :, 0:128], local.at[5])

    drain(s_in.at[0:per_device, 0:992], s_landed)
    for copy in own_rounds:
        copy.wait()
    for e in range(per_device):
        @pl.loop(0, 8)
        def _(k):
            s_turned[:, lanes(k)] = s_in[e, pl.ds(pl.multiple_of(k * 128, 128), 128), 0, :].T

        def store(columns, value):
            s_rotated[:, columns] = value

        rotate(s_turned[...], high, low, store)

        @pl.loop(0, 8)
        def _(k):
            s_out[e, pl.ds(pl.multiple_of(k * 128, 128), 128), 0, :] = s_rotated[:, lanes(k)].T

    @pl.loop(1, ROWS)
    def _(d):
        other = (row + d) % ROWS
        for e in range(per_device):
            send(
                s_out.at[e, pl.ds(other * 32, 32)],
                so_ref.at[:, first_round + row * per_device + e],
                so_sent, so_landed, (other, mine),
            )

    own_results = [
        pltpu.make_async_copy(
            s_out.at[e, pl.ds(row * 32, 32)], so_ref.at[:, first_round + row * per_device + e], local.at[6 + e]
        )
        for e in range(per_device)
    ]
    for copy in own_results:
        copy.start()

    own[2].wait()
    drain(c_in.at[0:chunks, :, 0:896], c_landed)
    turn(chunks, c_in, c_out, co_ref, out_sent.at[1], co_landed)
    drain(c_out.at[0:chunks, :, 0:128], local.at[5])

    for copy in own_results:
        copy.wait()
    drain(factor.at[0, 0, 0, :, 0:896], f_sent)
    for side in range(2):
        drain(factor.at[0, 0:3, 0, :, left], ring_sent.at[side])
        drain(factor.at[0:3, :, 0, :, left], far_sent.at[side])
    drain(factor.at[:, :, 0], pair_sent)
    drain(z_in.at[:, :, 0:896], in_sent.at[0])
    drain(c_in.at[0:chunks, :, 0:896], in_sent.at[1])
    drain(s_in.at[0:per_device, 0:992], s_sent)
    drain(s_in.at[0:per_device, 0:992], so_sent)
    drain(s_in.at[0:per_device, 0:992], so_landed)
    drain(z_out.at[:, :, 0:896], out_sent.at[0])
    drain(c_out.at[0:chunks, :, 0:896], out_sent.at[1])
    drain(z_out.at[:, :, 0:896], zo_landed)
    drain(c_out.at[0:chunks, :, 0:896], co_landed)


def variant(chunks):
    per_device, first_round = (2, 0) if chunks <= 2 else (1, 32)
    anywhere = pl.BlockSpec(memory_space=pl.ANY)
    blocks = jax.ShapeDtypeStruct((4, Z, CHUNK, 128), jnp.float32)
    dma = pltpu.SemaphoreType.DMA
    return pl.pallas_call(
        functools.partial(kernel, chunks, per_device, first_round),
        name=f"window_{chunks}",
        out_shape=(blocks, blocks, jax.ShapeDtypeStruct((32, 64, 1, 128), jnp.float32)),
        in_specs=[
            pl.BlockSpec(memory_space=pltpu.SMEM), pl.BlockSpec(memory_space=pltpu.VMEM),
            anywhere, anywhere, anywhere,
        ],
        out_specs=(anywhere, anywhere, anywhere),
        scratch_shapes=[
            pltpu.VMEM((4, 4, 2, 32, W), jnp.float32),
            pltpu.VMEM((W, W), jnp.bfloat16),
            pltpu.VMEM((W, W), jnp.bfloat16),
            *[pltpu.VMEM((4, CHUNK, W), jnp.float32) for _ in range(4)],
            *[pltpu.VMEM((2, W, 1, 128), jnp.float32) for _ in range(2)],
            *[pltpu.VMEM((128, W), jnp.float32) for _ in range(2)],
            dma((8,)),
            dma, dma, dma((2,)), dma((2,)), dma((2,)), dma((2, 4)), dma, dma,
            dma((2,)), dma, dma, dma((2,)), dma, dma, dma, dma, dma, dma,
        ],
        compiler_params=pltpu.CompilerParams(
            collective_id=chunks, has_side_effects=True, vmem_limit_bytes=48 * 1024 * 1024
        ),
    )


def body(vectors_window, column_strip, row_strip, factor, window_start, deflated):
    start = window_start[0]
    strip_blocks = column_strip.reshape(4, Z, CHUNK, 128)
    operands = (deflated, factor, vectors_window.reshape(4, Z, CHUNK, 128), strip_blocks, row_strip)
    vectors, strip, rows = lax.switch(
        (start - 1) // 16384, [variant(chunks) for chunks in (1, 2, 3, 4)], *operands
    )
    shape = (32, 1, 64, 128)
    row_number = (
        (lax.broadcasted_iota(jnp.int32, shape, 0) * ROWS + lax.axis_index("row")) * 64
        + lax.broadcasted_iota(jnp.int32, shape, 2)
    )
    column_updated = jnp.where(row_number < start, strip.reshape(shape), column_strip)
    column_number = (
        (lax.broadcasted_iota(jnp.int32, row_strip.shape, 1) * Z + lax.axis_index("col")) * 128
        + lax.broadcasted_iota(jnp.int32, row_strip.shape, 3)
    )
    row_updated = jnp.where(column_number >= start + W, rows, row_strip)
    return vectors.reshape(shape), column_updated, row_updated


def solution(mesh):
    return jax.shard_map(
        body,
        mesh=mesh,
        in_specs=(
            P(None, "row", None, "col"),
            P(None, "row", None, "col"),
            P("row", None, "col", None),
            P("row", "col"),
            P(),
            P(),
        ),
        out_specs=(
            P(None, "row", None, "col"),
            P(None, "row", None, "col"),
            P("row", None, "col", None),
        ),
        check_vma=False,
    )
```

time: 233 us -> 105 us (0.45)
  Pallas kernels: 0 us -> 95.7 us
  waiting for transfers between devices: 69.7 us -> 0 us
  local copies, waits for them, and re-layouts: 54.5 us -> 1.67 us
  starting transfers between devices: 30.3 us -> 0 us
  matrix products: 25.2 us -> 0 us
  between operations: 18.2 us -> 1.34 us
  blocking collectives: 16.6 us -> 0 us
  other arithmetic: 17.4 us -> 5.69 us
    pallas_call x0 -> x1, Pallas kernels: none -> 95.7 us  [body(): lax.switch((start - 1) // 16384, [variant(chunks) for chunks in (1, 2, 3,...]
    all_to_all x6 -> x0, waiting for transfers between devices: 53.6 us -> none  [the longest x1 14.1 us: body(): lax.all_to_all(flat_strip, 'row', split_axis=1, concat_axis=0, tiled=True)]
    all_to_all x6 -> x0, starting transfers between devices: 30.3 us -> none  [the longest x1 9.38 us: body(): lax.all_to_all(flat_strip, 'row', split_axis=1, concat_axis=0, tiled=True)]
    dot_general x4 -> x0, matrix products: 25.2 us -> none  [the longest x1 6.57 us: body(): lax.dot_general(rotation, stacked, (((0,), (0,)), ((), ())), precision=hi...]
    unnamed x19 -> x5, local copies, waits for them, and re-layouts: 22.3 us -> 1.67 us
    all_to_all x10 -> x0, local copies, waits for them, and re-layouts: 16.8 us -> none  [the longest x2 4.44 us: body(): lax.all_to_all(z_turned, 'col', split_axis=2, concat_axis=1, tiled=True)]
    all_to_all x1 -> x0, blocking collectives: 16.6 us -> none  [from_everyone(): lax.all_to_all(jnp.broadcast_to(x[None], (peers, *x.shape)), axis, 0, 0,...]
    all_gather x1 -> x0, waiting for transfers between devices: 16 us -> none  [body(): lax.all_gather(widened, 'row', axis=0, tiled=True)]
  transfers between devices with their start and end apart: 7 -> 0, of which waited for: 6 -> 0; matrix products, arithmetic and copies ran while one was open for 34% -> 0% of each run, Pallas kernels for 0% -> 0%
where the time goes in v1:
time: 105 us
  Pallas kernels  95.7 us (91%)
  other arithmetic  5.69 us (5%)
  local copies, waits for them, and re-layouts  1.67 us (2%)
  between operations  1.34 us (1%)
    pallas_call x1, Pallas kernels, body(): lax.switch((start - 1) // 16384, [variant(chunks) for chunks in (1, 2, 3,...  95.7 us
    select_n x1, other arithmetic, body(): row_updated = jnp.where(column_number >= start + W, rows, row_strip)  4.52 us

profile of v1, /device:TPU:1, one launch (start us, length us, event | category | flops | bytes accessed | tf_op | source)
XLA Modules:
  0.0 104.8 jit_solution(9379736882886478634)
XLA Ops:
  1.3 0.0 copy-start.1
  1.3 0.7 copy-done.1
  2.0 96.1 %conditional.1 = ((f32[4,8,64,128]{3,2,1,0:T(8,128)S(1)}, f32[4,8,64,128]{3,2,1,0:T(8,128)S(1)}, f32[32,64,1,128]{3,2,1,0:T(1,128)})) conditional(s32[]{:T(128)} %clamp.3, (s32[1]{0:T(128)}, f32[32,128]{1,0:T(8,128)S(1)}, f32[4,8,64,128]{3,2,1,0:T(8,128)}, f32[4,8,64,128]{3,2,1,0:T(8,128)}, ...), branch_computations={%region_0.1_spmd, %region_1.2_spmd, %region_2.3_spmd, %region_3.4_... | conditional | bytes 8 | solution.py:271
  2.0 95.7 %window_3.1 = (f32[4,8,64,128]{3,2,1,0:T(8,128)S(1)}, f32[4,8,64,128]{3,2,1,0:T(8,128)S(1)}, f32[32,64,1,128]{3,2,1,0:T(1,128)}) custom-call(s32[1]{0:T(128)} %get-tuple-element.70.deflated, f32[32,128]{1,0:T(8,128)S(1)} %get-tuple-element.71.f_ref, f32[4,8,64,128]{3,2,1,0:T(8,128)} %get-tuple-element.72.z_ref, f32[4,8,64,128]{3,2,1,0:T(8,128)} %get-tuple-element.73.c_ref, ...), custom_call_target="tpu_custom_call" | custom-call | tf_op jit(solution)/shard_map/cond/branch_2_fun/window_3/pallas_call | solution.py:271
  98.1 0.0 copy-start
  98.2 4.5 %compare_select_fusion = f32[32,64,1,128]{3,2,1,0:T(1,128)} fusion(f32[32,64,1,128]{3,2,1,0:T(1,128)} %get-tuple-element.101, f32[32,64,1,128]{3,2,1,0:T(1,128)} %param.12, s32[64]{0:T(128)S(1)} %add_multiply_fusion, s32[]{:T(128)S(6)} %add.51), kind=kLoop, calls=%fused_computation | loop fusion | flops 786432 | bytes 3145988 | tf_op jit(solution)/shard_map/jit(_where)/select_n | solution.py:284
  102.7 0.0 copy-done
  102.7 1.2 %fusion = f32[32,1,64,128]{3,2,1,0:T(8,128)} fusion(f32[32,1,64,128]{3,2,1,0:T(8,128)S(1)} %bitcast.21, f32[32,1,64,128]{3,2,1,0:T(8,128)S(1)} %copy-done, s32[]{:T(128)} %bitcast.10, s32[32]{0:T(128)S(1)} %add_multiply_fusion.1), kind=kLoop, calls=%fused_computation.2 | loop fusion | flops 786432 | bytes 3145860 | tf_op jit(solution)/shard_map/jit(_where)/select_n | solution.py:279
  103.8 1.0 copy.25
  (2 shorter events, 0.0 us)
Async XLA Ops:
  1.3 0.7 copy-start.1
  98.1 4.5 %copy-start = (f32[32,1,64,128]{3,2,1,0:T(8,128)S(1)}, f32[32,1,64,128]{3,2,1,0:T(8,128)}, u32[]{:S(2)}) copy-start(f32[32,1,64,128]{3,2,1,0:T(8,128)} %param.11) | copy-start | bytes 3145732

commit v2 on v1

v2 whole, which is shorter than its diff:
```python
import functools

import jax
import jax.numpy as jnp
from jax import lax
from jax.experimental import pallas as pl
from jax.experimental.pallas import tpu as pltpu
from jax.sharding import PartitionSpec as P

W = 1024
Z = 8
ROWS = 32
ROUNDS = 32
STEP = 4
MESH = pl.DeviceIdType.MESH


def send(src, dst, sent, landed, device):
    pltpu.make_async_remote_copy(
        src_ref=src, dst_ref=dst, send_sem=sent, recv_sem=landed, device_id=device, device_id_type=MESH
    ).start()


def drain(ref, semaphore):
    pltpu.make_async_copy(ref, ref, semaphore).wait()


def lanes(index, size=128):
    return pl.ds(pl.multiple_of(index * size, size), size)


def row_of(y, x, core):
    return (y * 4 + x) * 2 + core


def rotate(x, high, low, store):
    rows = x.shape[0]
    x_high = x.astype(jnp.bfloat16)
    x_low = (x - x_high.astype(jnp.float32)).astype(jnp.bfloat16)
    both = jnp.concatenate([x_high, x_low], axis=0)
    for n in range(4):
        columns = slice(256 * n, 256 * n + 256)
        top = jnp.dot(both, high[:, columns], preferred_element_type=jnp.float32)
        bottom = jnp.dot(x_high, low[:, columns], preferred_element_type=jnp.float32)
        store(columns, top[:rows] + top[rows:] + bottom)


def kernel(
    rounds, per_device, first_round,
    starts, deflated, f_ref, z_ref, c_ref, s_ref,
    zo_ref, co_ref, so_ref,
    factor, high, low, z_in, c_in, z_out, c_out, s_in, s_out, s_turned, s_rotated,
    local, f_sent, f_landed, ring_sent, ring_landed, far_sent, far_landed, pair_sent, pair_landed,
    in_sent, z_landed, c_landed, out_sent, zo_landed, co_landed, s_sent, s_landed, so_sent, so_landed,
):
    row = lax.axis_index("row")
    mine = lax.axis_index("col")
    y, x, core = row // 8, (row // 2) % 4, row % 2
    barrier = pltpu.get_barrier_semaphore()
    own_factor = factor.at[y, x, core, :, lanes(mine)]
    load = pltpu.make_async_copy(f_ref, own_factor, local.at[0])
    load.start()

    @pl.loop(1, Z)
    def _(d):
        pl.semaphore_signal(barrier, inc=1, device_id=(row, (mine + d) % Z), device_id_type=MESH)

    @pl.loop(1, ROWS)
    def _(d):
        pl.semaphore_signal(barrier, inc=1, device_id=((row + d) % ROWS, mine), device_id_type=MESH)

    start = starts[0]
    untouched = []
    if rounds < ROUNDS:
        untouched.append((c_ref.at[rounds:], co_ref.at[rounds:]))
    if first_round:
        untouched.append((s_ref.at[:, 0:first_round], so_ref.at[:, 0:first_round]))
    own = [
        pltpu.make_async_copy(z_ref.at[:, mine], z_in.at[:, :, lanes(mine)], local.at[1]),
        pltpu.make_async_copy(c_ref.at[0:rounds, mine], c_in.at[0:rounds, :, lanes(mine)], local.at[2]),
    ]
    for copy in own:
        copy.start()
    kept = [pltpu.make_async_copy(source, target, local.at[8 + n]) for n, (source, target) in enumerate(untouched)]
    load.wait()
    pl.semaphore_wait(barrier, Z - 1 + ROWS - 1)

    far_first = (4, 3, 5, 2, 6, 1, 7)
    for d in far_first:
        send(own_factor, own_factor, f_sent, f_landed, (row, (mine + d) % Z))
    for d in far_first:
        other = (mine + d) % Z
        send(z_ref.at[:, other], z_in.at[:, :, lanes(mine)], in_sent.at[0], z_landed, (row, other))
    for copy in kept:
        copy.start()
    for d in far_first:
        other = (mine + d) % Z
        send(
            c_ref.at[0:rounds, other], c_in.at[0:rounds, :, lanes(mine)],
            in_sent.at[1], c_landed, (row, other),
        )

    left, right = slice(0, 512), slice(512, 1024)
    partner = (row_of(y, x, 1 - core), mine)

    def along_x(d):
        return row_of(y, (x + d) % 4, core), mine

    def along_y(d):
        return row_of((y + d) % 4, x, core), mine

    drain(factor.at[0, 0, 0, :, 0:896], f_landed)
    piece_left, piece_right = factor.at[y, x, core, :, left], factor.at[y, x, core, :, right]
    for d in (2, 1, 3):
        send(piece_left, piece_left, ring_sent.at[0], ring_landed.at[0, d], along_x(d))
        send(piece_right, piece_right, ring_sent.at[1], ring_landed.at[1, d], along_y(d))
    for d in (2, 1, 3):
        send(piece_left, piece_left, far_sent.at[0], far_landed.at[0, d], along_y(d))
        send(piece_right, piece_right, far_sent.at[1], far_landed.at[1, d], along_x(d))
    send(piece_left, piece_left, pair_sent, pair_landed, partner)
    send(piece_right, piece_right, pair_sent, pair_landed, partner)
    for e in (1, 3, 2):
        piece_left = factor.at[y, (x + 4 - e) % 4, core, :, left]
        drain(piece_left, ring_landed.at[0, e])
        for d in (2, 1, 3):
            send(piece_left, piece_left, far_sent.at[0], far_landed.at[0, d], along_y(d))
        piece_right = factor.at[(y + 4 - e) % 4, x, core, :, right]
        drain(piece_right, ring_landed.at[1, e])
        for d in (2, 1, 3):
            send(piece_right, piece_right, far_sent.at[1], far_landed.at[1, d], along_x(d))
        send(piece_left, piece_left, pair_sent, pair_landed, partner)
        send(piece_right, piece_right, pair_sent, pair_landed, partner)

    @pl.loop(1, ROWS)
    def _(d):
        other = (row + d) % ROWS
        for e in range(per_device):
            send(
                s_ref.at[:, first_round + other * per_device + e],
                s_in.at[e, pl.ds(row * 32, 32)],
                s_sent, s_landed, (other, mine),
            )

    own_rounds = [
        pltpu.make_async_copy(
            s_ref.at[:, first_round + row * per_device + e], s_in.at[e, pl.ds(row * 32, 32)], local.at[3 + e]
        )
        for e in range(per_device)
    ]
    for copy in own_rounds:
        copy.start()

    for d in (1, 3, 2):
        line = factor.at[(y + 4 - d) % 4, :, core, :, left]
        drain(line, far_landed.at[0, d])
        send(line, line, pair_sent, pair_landed, partner)
        line = factor.at[:, (x + 4 - d) % 4, core, :, right]
        drain(line, far_landed.at[1, d])
        send(line, line, pair_sent, pair_landed, partner)
    drain(factor.at[:, :, 0], pair_landed)

    spike = factor[0, 0, 0, 0:1, :]
    columns = lax.broadcasted_iota(jnp.int32, (1, W), 1)
    spike_row = jnp.where(columns < W - deflated[0], spike, 0.0)
    squares = jnp.sum(spike_row * spike_row, axis=1, keepdims=True)
    corner = spike[:, 0:1]
    magnitude = jnp.sqrt(squares + 1e-06)
    signum = jnp.where(corner >= 0, 1.0, -1.0)
    vector = spike_row + jnp.where(columns == 0, signum * magnitude, 0.0)
    denominator = squares + 2.0 * jnp.abs(corner) * magnitude + magnitude * magnitude
    scaling = 2.0 / denominator

    @pl.loop(0, ROWS, unroll=4)
    def _(b):
        block = factor[b // 8, (b // 2) % 4, b % 2]
        image = jnp.sum(block * vector, axis=1, keepdims=True)
        turned = block - (scaling * image) * vector
        top = turned.astype(jnp.bfloat16)
        high[pl.ds(pl.multiple_of(b * 32, 32), 32), :] = top
        low[pl.ds(pl.multiple_of(b * 32, 32), 32), :] = (turned - top.astype(jnp.float32)).astype(jnp.bfloat16)

    def turn_some(first, count, source, result, target, sent, landed, bounded):
        some = pl.ds(first, count)
        shape = (count, 8, 256)
        number = (
            ((first + lax.broadcasted_iota(jnp.int32, shape, 0)) * ROWS + row) * 64
            + mine * 8 + lax.broadcasted_iota(jnp.int32, shape, 1)
        )

        def store(columns, value):
            value = value.reshape(shape)
            if bounded:
                value = jnp.where(number < start, value, source[some, :, columns])
            result[some, :, columns] = value

        rotate(source[some].reshape(count * 8, W), high, low, store)
        for d in far_first:
            other = (mine + d) % Z
            send(result.at[some, :, lanes(other)], target.at[some, mine], sent, landed, (row, other))
        pltpu.make_async_copy(result.at[some, :, lanes(mine)], target.at[some, mine], local.at[5]).start()

    def turn(count, *where):
        if count >= 8:
            @pl.loop(0, count // 8)
            def _(c):
                turn_some(pl.multiple_of(c * 8, 8), 8, *where)

        if count % 8:
            turn_some(count - count % 8, count % 8, *where)

    own[0].wait()
    drain(z_in.at[:, :, 0:896], z_landed)
    turn(ROUNDS, z_in, z_out, zo_ref, out_sent.at[0], zo_landed, False)
    drain(z_out.at[:, :, 0:128], local.at[5])

    drain(s_in.at[0:per_device, 0:992], s_landed)
    for copy in own_rounds:
        copy.wait()
    for e in range(per_device):
        @pl.loop(0, 8)
        def _(k):
            s_turned[:, lanes(k)] = s_in[e, pl.ds(pl.multiple_of(k * 128, 128), 128), 0, :].T

        number = (
            ((first_round + row * per_device + e) * Z + mine) * 128
            + lax.broadcasted_iota(jnp.int32, (128, 256), 0)
        )

        def store(columns, value):
            s_rotated[:, columns] = jnp.where(number >= start + W, value, s_turned[:, columns])

        rotate(s_turned[...], high, low, store)

        @pl.loop(0, 8)
        def _(k):
            s_out[e, pl.ds(pl.multiple_of(k * 128, 128), 128), 0, :] = s_rotated[:, lanes(k)].T

    @pl.loop(1, ROWS)
    def _(d):
        other = (row + d) % ROWS
        for e in range(per_device):
            send(
                s_out.at[e, pl.ds(other * 32, 32)],
                so_ref.at[:, first_round + row * per_device + e],
                so_sent, so_landed, (other, mine),
            )

    own_results = [
        pltpu.make_async_copy(
            s_out.at[e, pl.ds(row * 32, 32)], so_ref.at[:, first_round + row * per_device + e], local.at[6 + e]
        )
        for e in range(per_device)
    ]
    for copy in own_results:
        copy.start()

    own[1].wait()
    drain(c_in.at[0:rounds, :, 0:896], c_landed)
    turn(rounds, c_in, c_out, co_ref, out_sent.at[1], co_landed, True)
    drain(c_out.at[0:rounds, :, 0:128], local.at[5])

    for copy in own_results + kept:
        copy.wait()
    drain(factor.at[0, 0, 0, :, 0:896], f_sent)
    for side in range(2):
        drain(factor.at[0, 0:3, 0, :, left], ring_sent.at[side])
        drain(factor.at[0:3, :, 0, :, left], far_sent.at[side])
    drain(factor.at[:, :, 0], pair_sent)
    drain(z_in.at[:, :, 0:896], in_sent.at[0])
    drain(c_in.at[0:rounds, :, 0:896], in_sent.at[1])
    drain(s_in.at[0:per_device, 0:992], s_sent)
    drain(s_in.at[0:per_device, 0:992], so_sent)
    drain(s_in.at[0:per_device, 0:992], so_landed)
    drain(z_out.at[:, :, 0:896], out_sent.at[0])
    drain(c_out.at[0:rounds, :, 0:896], out_sent.at[1])
    drain(z_out.at[:, :, 0:896], zo_landed)
    drain(c_out.at[0:rounds, :, 0:896], co_landed)


def variant(rounds):
    per_device, first_round = (2, 0) if rounds <= 16 else (1, 32)
    anywhere = pl.BlockSpec(memory_space=pl.ANY)
    blocks = jax.ShapeDtypeStruct((ROUNDS, Z, 8, 128), jnp.float32)
    dma = pltpu.SemaphoreType.DMA
    return pl.pallas_call(
        functools.partial(kernel, rounds, per_device, first_round),
        name=f"window_{rounds}",
        out_shape=(blocks, blocks, jax.ShapeDtypeStruct((32, 64, 1, 128), jnp.float32)),
        in_specs=[*[pl.BlockSpec(memory_space=pltpu.SMEM)] * 2, *[pl.BlockSpec(memory_space=pltpu.HBM)] * 4],
        out_specs=(anywhere, anywhere, anywhere),
        scratch_shapes=[
            pltpu.VMEM((4, 4, 2, 32, W), jnp.float32),
            pltpu.VMEM((W, W), jnp.bfloat16),
            pltpu.VMEM((W, W), jnp.bfloat16),
            *[pltpu.VMEM((ROUNDS, 8, W), jnp.float32) for _ in range(4)],
            *[pltpu.VMEM((2, W, 1, 128), jnp.float32) for _ in range(2)],
            *[pltpu.VMEM((128, W), jnp.float32) for _ in range(2)],
            dma((10,)),
            dma, dma, dma((2,)), dma((2, 4)), dma((2,)), dma((2, 4)), dma, dma,
            dma((2,)), dma, dma, dma((2,)), dma, dma, dma, dma, dma, dma,
        ],
        compiler_params=pltpu.CompilerParams(
            collective_id=rounds // STEP, has_side_effects=True, vmem_limit_bytes=48 * 1024 * 1024
        ),
    )


def body(vectors_window, column_strip, row_strip, factor, window_start, deflated):
    start = window_start[0]
    by_worker = (ROUNDS, Z, 8, 128)
    vectors, strip, rows = lax.switch(
        (start - 1) // (64 * ROWS * STEP),
        [variant(rounds) for rounds in range(STEP, ROUNDS + 1, STEP)],
        window_start, deflated, factor,
        vectors_window.reshape(by_worker), column_strip.reshape(by_worker), row_strip,
    )
    return vectors.reshape(vectors_window.shape), strip.reshape(column_strip.shape), rows


def solution(mesh):
    return jax.shard_map(
        body,
        mesh=mesh,
        in_specs=(
            P(None, "row", None, "col"),
            P(None, "row", None, "col"),
            P("row", None, "col", None),
            P("row", "col"),
            P(),
            P(),
        ),
        out_specs=(
            P(None, "row", None, "col"),
            P(None, "row", None, "col"),
            P("row", None, "col", None),
        ),
        check_vma=False,
    )
```

time: 105 us -> 107 us (1.019)
  other arithmetic: 5.69 us -> 0 us
  Pallas kernels: 95.7 us -> 101 us
  local copies, waits for them, and re-layouts: 1.67 us -> 3.6 us
    pallas_call x1, Pallas kernels: 95.7 us -> 101 us  [body(): lax.switch((start - 1) // (64 * ROWS * STEP), [variant(rounds) for rounds...]
    select_n x2 -> x0, other arithmetic: 5.68 us -> none  [the longest x1 4.52 us: body(): row_updated = jnp.where(column_number >= start + W, rows, row_strip)]
    unnamed x5, local copies, waits for them, and re-layouts: 1.67 us -> 3.6 us
where the time goes in v2:
time: 107 us
  Pallas kernels  101 us (94%)
  local copies, waits for them, and re-layouts  3.6 us (3%)
  between operations  1.32 us (1%)
    pallas_call x1, Pallas kernels, body(): lax.switch((start - 1) // (64 * ROWS * STEP), [variant(rounds) for rounds...  101 us
    unnamed x5, local copies, waits for them, and re-layouts  3.6 us

profile of v2, /device:TPU:1, one launch (start us, length us, event | category | flops | bytes accessed | tf_op | source)
XLA Modules:
  0.0 106.9 jit_solution(9393218366623556782)
XLA Ops:
  1.3 0.0 copy-start
  1.3 0.7 copy-done
  2.0 102.0 %conditional.1 = ((f32[32,8,8,128]{3,2,1,0:T(8,128)S(1)}, f32[32,8,8,128]{3,2,1,0:T(8,128)S(1)}, f32[32,64,1,128]{3,2,1,0:T(1,128)S(1)})) conditional(s32[]{:T(128)} %clamp.3, (s32[1]{0:T(128)}, s32[1]{0:T(128)}, f32[32,128]{1,0:T(8,128)S(1)}, f32[32,8,8,128]{3,2,1,0:T(8,128)}, f32[32,8,8,128]{3,2,1,0:T(8,128)}, ...), branch_computations={%region_0.1_spmd, %region_1.2_spmd, %region_2.3_spmd, %region_3.4_... | conditional | bytes 8 | solution.py:311
  2.0 101.4 %window_28.1 = (f32[32,8,8,128]{3,2,1,0:T(8,128)S(1)}, f32[32,8,8,128]{3,2,1,0:T(8,128)S(1)}, f32[32,64,1,128]{3,2,1,0:T(1,128)S(1)}) custom-call(s32[1]{0:T(128)} %get-tuple-element.176.starts, s32[1]{0:T(128)} %get-tuple-element.177.deflated, f32[32,128]{1,0:T(8,128)S(1)} %get-tuple-element.178.f_ref, f32[32,8,8,128]{3,2,1,0:T(8,128)} %get-tuple-element.179.z_ref, ...), custom_call_target="tpu_custom_call" | custom-call | tf_op jit(solution)/shard_map/cond/branch_6_fun/window_28/pallas_call | solution.py:311
  104.0 1.0 copy.39
  105.0 1.0 copy.40
  106.0 1.0 copy.41
Async XLA Ops:
  1.3 0.7 copy-start
